TPU v7x, 256 devices: a whole 4x4x8 slice. The times are simulated.
256 devices in a mesh: aux: 64 (over x, z, core), pair: 4 (over y).
Axes of the slice: x: 4, y: 4, z: 8, core: 2. Of those that a mesh axis runs over, the one named last changes fastest.
Arguments:
- three_centre: bfloat16 [16, 1280, 128, 128], P('pair', 'aux'), may hold values from -6 to 6
- block_mask: int32 [16], replicated, may hold values from 0 to 1, as said below
- block_owner: int32 [16], replicated, may hold values from 0 to 3, as said below
- block_index: int32 [2, 16], replicated, may hold values from 0 to 23
- active_orbitals: bfloat16 [24, 3072], replicated, may hold values from -0.5 to 0.5
- inactive_orbitals: bfloat16 [256, 3072], replicated, may hold values from -0.75 to 0.75
Outputs:
- fock_blocks: float32 [32, 128, 128], P('pair')
- active_integrals: float32 [576, 576], P('aux')
Inputs may be any that keep to these rules, and one draw needn't show every extreme that they name: `block_mask`: every index of pair holds at least 2 live slots. `block_owner`: among the 4 slots of one index of pair, live or not, at most 2 name any one owner; one owner is named by exactly 2 live slots of every index of pair, so it receives 8 live blocks.
All inputs are finite; a program needn't handle non-finite values.
Results may differ from a plain program's by a relative error of at most 0.0044.
Values may be sent and summed in bfloat16 or wider, within the bound.
No kernel may reach another device: no remote copies, remote signals or barrier semaphores. Data moves between devices by JAX's collectives and lax.ppermute only.
A program may use at most 64 MiB of HBM per device.

v0:
```python
import math

import jax
import jax.numpy as jnp
from jax import lax
from jax.sharding import PartitionSpec as P


def sent_to_all(x, axis):
    count = lax.axis_size(axis)
    return lax.all_to_all(jnp.broadcast_to(x[None], (count, *x.shape)), axis, 0, 0, tiled=True)


def of_everyone(x, axis):
    return sent_to_all(x, axis).sum(axis=0)


def together(arrays, axis):
    ends = [0]
    for a in arrays:
        ends.append(ends[-1] + a.size)
    total = of_everyone(jnp.concatenate([a.ravel() for a in arrays]), axis)
    return tuple((total[b:e].reshape(a.shape) for a, b, e in zip(arrays, ends, ends[1:])))


def rows_for(lines, count):
    spare = -len(lines) % count
    return jnp.pad(lines, [(0, spare)] + [(0, 0)] * (lines.ndim - 1))


def joined_along(pieces, dim):
    pieces = jnp.moveaxis(pieces, 0, dim)
    lengths = pieces.shape
    return pieces.reshape(*lengths[:dim], lengths[dim] * lengths[dim + 1], *lengths[dim + 2 :])


def gathered_copies(x, axis, dim):
    pieces = sent_to_all(x, axis)
    return joined_along(pieces, dim)


def split_up(x, dim, count):
    before, after = (x.shape[:dim], x.shape[dim + 1 :])
    return jnp.moveaxis(x.reshape(*before, count, -1, *after), dim, 0)


def sent_and_summed(x, axis, dim):
    count = lax.axis_size(axis)
    pieces = lax.all_to_all(split_up(x, dim, count), axis, 0, 0, tiled=True)
    return jnp.sum(pieces, axis=0)


def total_of(x, axes):
    lines = x.reshape(-1, x.shape[-1])
    padded = rows_for(lines, lax.axis_size(axes))
    whole = gathered_copies(sent_and_summed(padded, axes, 0), axes, 0)
    return lax.slice_in_dim(whole, 0, len(lines)).reshape(x.shape)


def owner_tables(block_mask, block_owner, slot_count, pair_count):
    owners = jnp.arange(pair_count, dtype=jnp.int32)
    flagged = ((block_owner[:, None] == owners[None, :]) & (block_mask[:, None] == 1)).astype(
        jnp.int32
    )
    global_rank = jnp.sum((jnp.cumsum(flagged, axis=0) - flagged) * flagged, axis=1)
    per_source = flagged.reshape(pair_count, slot_count, pair_count)
    source_rank = jnp.sum((jnp.cumsum(per_source, axis=1) - per_source) * per_source, axis=2)
    slot_places = jnp.arange(slot_count // 2, dtype=jnp.int32)
    matches = (source_rank[:, None, None, :] == slot_places[None, None, :, None]).astype(jnp.int32)
    chosen = jnp.transpose(per_source, (0, 2, 1))[:, :, None, :] * matches
    return (global_rank, chosen)


def slot_pick(route_table, slot_count):
    positions = jnp.arange(slot_count, dtype=jnp.int32)
    return (jnp.sum(route_table * positions, axis=-1), jnp.sum(route_table, axis=-1))


def fitted_terms(blocks, living, row_blocks, col_blocks, active_split, inactive_split, block_width):
    active_rows = jnp.take(active_split, row_blocks, axis=1)
    active_cols = jnp.take(active_split, col_blocks, axis=1)
    half_done = jnp.einsum(
        "rpab,urb->rpua", blocks, active_cols, preferred_element_type=jnp.float32
    ).astype(jnp.bfloat16)
    weighted = active_rows * living.astype(jnp.bfloat16)[None, :, None]
    fitted = jnp.einsum("rpua,tra->ptu", half_done, weighted, preferred_element_type=jnp.float32)
    inactive_rows = jnp.take(inactive_split, row_blocks, axis=1)
    inactive_cols = jnp.take(inactive_split, col_blocks, axis=1)
    density = jnp.einsum(
        "kra,krb->rab", inactive_rows, inactive_cols, preferred_element_type=jnp.float32
    ).astype(jnp.bfloat16)
    density = density * living.astype(jnp.bfloat16)[:, None, None]
    coupling = (
        jnp.einsum("rpab,rab->p", blocks, density, preferred_element_type=jnp.float32) / block_width
    )
    return (fitted.reshape(fitted.shape[0], -1), coupling)


def shards(three_centre, block_mask, block_owner, block_index, active_orbitals, inactive_orbitals):
    slot_count = three_centre.shape[0]
    aux_rows = three_centre.shape[1]
    block_width = three_centre.shape[2]
    pair_count = lax.axis_size("pair")
    aux_count = lax.axis_size("aux")
    total_aux = aux_count * aux_rows
    pair_here = lax.axis_index("pair")
    capacity = slot_count // 2
    active_split = active_orbitals.reshape(active_orbitals.shape[0], -1, block_width)
    inactive_split = inactive_orbitals.reshape(inactive_orbitals.shape[0], -1, block_width)
    global_rank, chosen = owner_tables(block_mask, block_owner, slot_count, pair_count)
    outgoing = jnp.take(chosen, pair_here, axis=0)
    incoming = jnp.take(chosen, pair_here, axis=1)
    send_slot, send_live = slot_pick(outgoing, slot_count)
    recv_slot, recv_live = slot_pick(incoming, slot_count)
    source_starts = jnp.arange(pair_count, dtype=jnp.int32)[:, None] * slot_count
    recv_global = (source_starts + recv_slot).reshape(-1)
    recv_live = recv_live.reshape(-1)
    send_flat = send_slot.reshape(-1)
    send_mask = send_live.reshape(-1)
    block_slots = pair_here * slot_count + jnp.arange(slot_count, dtype=jnp.int32)
    living = jnp.take(block_mask, block_slots)
    row_blocks = jnp.take(block_index[0], block_slots)
    col_blocks = jnp.take(block_index[1], block_slots)
    fitted_part, coupling_part = fitted_terms(
        three_centre, living, row_blocks, col_blocks, active_split, inactive_split, block_width
    )
    fitted_sum, coupling_sum = together((fitted_part, coupling_part), "pair")
    fitted = fitted_sum.astype(jnp.bfloat16)
    coupling = coupling_sum.astype(jnp.bfloat16)
    coulomb = jnp.einsum(
        "rpab,p->rab", three_centre, coupling, preferred_element_type=jnp.float32
    ) * (1.0 / math.sqrt(total_aux))
    outbound = jnp.take(coulomb, send_flat, axis=0) * send_mask.astype(jnp.float32)[:, None, None]
    outbound = outbound.reshape(pair_count, capacity, block_width, block_width)
    coulomb = lax.all_to_all(outbound, "pair", split_axis=0, concat_axis=0, tiled=True).reshape(
        pair_count * capacity, block_width, block_width
    )
    slot_rank = jnp.take(global_rank, recv_global)
    owned_slots = pair_count * capacity
    rank_values = jnp.arange(owned_slots, dtype=jnp.int32)
    selector = (slot_rank[None, :] == rank_values[:, None]).astype(jnp.float32) * recv_live.astype(
        jnp.float32
    )[None, :]
    fock_part = jnp.einsum("kr,rab->kab", selector, coulomb, precision=lax.Precision.HIGHEST)
    fock_blocks = total_of(fock_part, "aux")
    row_share = fitted.shape[1] // aux_count
    first_row = lax.axis_index("aux") * row_share
    portion = lax.all_gather(fitted, "aux", axis=0, tiled=True)
    own_cols = lax.dynamic_slice_in_dim(portion, first_row, row_share, 1)
    gram_block = jnp.dot(own_cols.T, portion, preferred_element_type=jnp.float32) / total_aux
    return (fock_blocks, gram_block)


def solution(mesh):
    return jax.shard_map(
        shards,
        mesh=mesh,
        in_specs=(P("pair", "aux", None, None), P(), P(), P(), P(), P()),
        out_specs=(P("pair", None, None), P("aux", None)),
        check_vma=False,
    )
```

profile of v0, /device:TPU:1, one launch (start us, length us, event | category | flops | bytes accessed | tf_op | source)
XLA Modules:
  0.0 136.8 jit_solution(12371279425353246228)
XLA Ops:
  7.2 0.9 slice_bitcast_fusion.3
  8.1 0.6 gather_fusion.5
  8.7 0.6 gather_fusion.2
  9.4 0.9 copy_bitcast_fusion
  10.3 0.6 gather_fusion.6
  10.9 0.6 gather_fusion.3
  11.4 2.6 %copy.42 = bf16[256,3072]{0,1:T(8,128)(2,1)} copy(bf16[256,3072]{1,0:T(8,128)(2,1)} %param.17) | data formatting | bytes 3145728 | tf_op args[5]
  14.1 2.6 %copy.43 = bf16[256,24,128]{2,0,1:T(8,128)(2,1)} copy(bf16[256,24,128]{0,2,1:T(8,128)(2,1)} %bitcast.79) | data formatting | bytes 3145728 | tf_op jit(solution)/shard_map/reshape | solution.py:109
  16.7 2.0 %gather_fusion.8 = bf16[4,256,128]{2,1,0:T(8,128)(2,1)S(1)} fusion(bf16[256,24,128]{2,0,1:T(8,128)(2,1)} %copy.43, s32[1024]{0:T(1024)S(1)} %pad_clamp_fusion.1), kind=kCustom, calls=%fused_computation.6.clone | custom fusion | bytes 524304 | tf_op jit(solution)/shard_map/jit(_take)/gather | solution.py:88
  18.7 2.0 %gather_fusion.7 = bf16[4,256,128]{2,1,0:T(8,128)(2,1)S(1)} fusion(bf16[256,24,128]{2,0,1:T(8,128)(2,1)} %copy.43, s32[1024]{0:T(1024)S(1)} %pad_clamp_fusion.2), kind=kCustom, calls=%fused_computation.2.clone | custom fusion | bytes 524304 | tf_op jit(solution)/shard_map/jit(_take)/gather | solution.py:87
  20.7 0.6 gather_fusion.4
  21.3 1.9 %fusion.15 = f32[20,24,24]{2,1,0:T(8,128)S(1)} fusion(bf16[4,20,128,128]{3,2,1,0:T(8,128)(2,1)S(1)} %copy-done, bf16[4,24,128]{2,1,0:T(8,128)(2,1)S(1)} %gather_fusion.6, bf16[4,24,128]{2,1,0:T(8,128)(2,1)S(1)} %gather_fusion.3, pred[4]{0:T(512)(128)(4,1)S(1)} %get-tuple-element.31, pred[4]{0:T(512)(128)(4,1)S(1)} %get-tuple-element.37, ...), kind=kOutput, calls=%fused_computation.18 | convolution fusion | flops 75030528 | bytes 2716688 | tf_op jit(solution)/shard_map/rpua,tra->ptu/dot_general | solution.py:86
  23.2 0.2 reshape_reshape.6
  23.4 0.4 fusion.19
  23.8 3.0 %fusion.23 = f32[20]{0:T(128)S(1)} fusion(bf16[4,20,128,128]{3,2,1,0:T(8,128)(2,1)S(1)} %copy-done, bf16[4,128,128,1]{2,1,0,3:T(8,128)(2,1)S(1)} %fusion.19), kind=kOutput, calls=%fused_computation.24 | convolution fusion | flops 2621460 | bytes 2752592 | tf_op jit(solution)/shard_map/rpab,rab->p/dot_general | solution.py:94
  26.8 0.8 broadcast_in_dim.82
  27.5 5.0 %all-to-all-start = ((f32[4,1,11540]{2,1,0:T(1,128)}), f32[4,1,11540]{2,1,0:T(1,128)S(1)}, u32[]{:S(2)}, u32[]{:S(2)}) async-start(f32[4,1,11540]{2,1,0:T(1,128)} %broadcast_in_dim.82), calls=%async_computation | async-start | bytes 372736 | tf_op jit(solution)/shard_map/all_to_all | solution.py:11
  32.6 0.1 and.60
  32.7 0.1 eq.64
  32.9 0.2 select_reduce_fusion.1
  33.2 0.2 fusion.57
  33.4 0.1 reshape.191
  33.6 0.1 add.92
  33.7 0.2 fusion.63
  33.8 3.8 %all-to-all-done = f32[4,1,11540]{2,1,0:T(1,128)S(1)} async-done(((f32[4,1,11540]{2,1,0:T(1,128)}), f32[4,1,11540]{2,1,0:T(1,128)S(1)}, u32[]{:S(2)}, u32[]{:S(2)}) %all-to-all-start) | async-done | bytes 184672 | tf_op jit(solution)/shard_map/all_to_all | solution.py:11
  37.7 0.2 reduce_sum.77
  37.9 2.2 %fusion = f32[1,4,128,128]{3,0,2,1:T(1,128)S(1)} fusion(bf16[4,20,128,128]{3,2,1,0:T(8,128)(2,1)S(1)} %copy-done, bf16[11540]{0:T(1024)(128)(2,1)S(1)} %reduce_sum.77), kind=kOutput, calls=%fused_computation.9 | convolution fusion | flops 2621440 | bytes 2884096 | tf_op jit(solution)/shard_map/rpab,p->rab/dot_general | solution.py:130
  40.0 0.7 reshape.339
  40.8 0.6 gather_fusion.1
  41.4 1.3 fusion.26
  42.7 3.5 %all-to-all-start.1 = ((f32[4,2,128,128]{3,1,2,0:T(2,128)}), f32[4,2,128,128]{3,1,2,0:T(2,128)S(1)}, u32[]{:S(2)}, u32[]{:S(2)}) async-start(f32[4,2,128,128]{3,1,2,0:T(2,128)} %fusion.26), calls=%async_computation.1 | async-start | bytes 1048576 | tf_op jit(solution)/shard_map/all_to_all | solution.py:135
  46.2 0.1 add.90
  46.3 0.1 fusion.62
  46.5 0.1 convert_element_type.58
  46.6 0.2 select_reduce_fusion
  46.8 0.7 gather_fusion
  47.4 5.7 %all-to-all-done.1 = f32[4,2,128,128]{3,1,2,0:T(2,128)S(1)} async-done(((f32[4,2,128,128]{3,1,2,0:T(2,128)}), f32[4,2,128,128]{3,1,2,0:T(2,128)S(1)}, u32[]{:S(2)}, u32[]{:S(2)}) %all-to-all-start.1) | async-done | bytes 524320 | tf_op jit(solution)/shard_map/all_to_all | solution.py:135
  53.1 0.2 copy.48
  53.3 0.6 fusion.55
  53.8 0.1 copy.49
  54.0 32.6 %all_to_all.21 = f32[64,16,128]{2,1,0:T(8,128)S(1)} all-to-all(f32[64,16,128]{2,1,0:T(8,128)S(1)} %bitcast.82), channel_id=1, replica_groups=mesh['aux'=64,'pair'=4] {'aux'}, dimensions={0} | all-to-all | bytes 1048576 | tf_op jit(solution)/shard_map/all_to_all | solution.py:49
  86.6 0.8 broadcast_in_dim.84
  87.5 6.1 %all-to-all-start.3 = ((f32[64,16,128]{2,1,0:T(8,128)}), f32[64,16,128]{2,1,0:T(8,128)S(1)}, u32[]{:S(2)}, u32[]{:S(2)}) async-start(f32[64,16,128]{2,1,0:T(8,128)} %broadcast_in_dim.84), calls=%async_computation.3 | async-start | bytes 1048576 | tf_op jit(solution)/shard_map/all_to_all | solution.py:11
  93.6 19.7 %all-to-all-done.3 = f32[64,16,128]{2,1,0:T(8,128)S(1)} async-done(((f32[64,16,128]{2,1,0:T(8,128)}), f32[64,16,128]{2,1,0:T(8,128)S(1)}, u32[]{:S(2)}, u32[]{:S(2)}) %all-to-all-start.3) | async-done | bytes 524320 | tf_op jit(solution)/shard_map/all_to_all | solution.py:11
  113.4 9.2 %all-gather.3.cloned.1.call-done = bf16[64,20,576]{2,1,0:T(8,128)(2,1)} async-done(((bf16[1,20,576]{2,1,0:T(8,128)(2,1)}), bf16[64,20,576]{2,1,0:T(8,128)(2,1)}) %all-gather.3.cloned.1.call-update) | async-done | bytes 1474576 | tf_op jit(solution)/shard_map/all_gather | solution.py:148
  122.6 3.9 %reshape.340 = bf16[1280,576]{1,0:T(8,128)(2,1)} reshape(bf16[64,20,576]{2,1,0:T(8,128)(2,1)} %all-gather.3.cloned.1.call-done) | data formatting | bytes 2949120
  126.4 2.7 %convolution_multiply_fusion = f32[9,576]{1,0:T(8,128)} fusion(bf16[1280,576]{1,0:T(8,128)(2,1)} %reshape.340, s32[]{:T(128)S(6)} %select_n.95), kind=kOutput, calls=%fused_computation.22 | convolution fusion | flops 13276224 | bytes 1986820 | tf_op jit(solution)/shard_map/dot_general | solution.py:150
  129.2 0.8 copy.85
  (33 shorter events, 0.6 us)
Async XLA Ops:
  7.2 14.2 %copy-start = (bf16[4,20,128,128]{3,2,1,0:T(8,128)(2,1)S(1)}, bf16[4,20,128,128]{3,2,1,0:T(8,128)(2,1)}, u32[]{:S(2)}) copy-start(bf16[4,20,128,128]{3,2,1,0:T(8,128)(2,1)} %param.12) | copy-start | bytes 7864324
  14.1 6.6 %copy-start.1 = (s32[16]{0:T(128)S(1)}, s32[16]{0:T(128)}, u32[]{:S(2)}) copy-start(s32[16]{0:T(128)} %param.13) | copy-start | bytes 196
  23.8 8.9 %copy-start.2 = (s32[16]{0:T(128)S(1)}, s32[16]{0:T(128)}, u32[]{:S(2)}) copy-start(s32[16]{0:T(128)} %param.14) | copy-start | bytes 196
  27.5 10.1 %all-to-all-start = ((f32[4,1,11540]{2,1,0:T(1,128)}), f32[4,1,11540]{2,1,0:T(1,128)S(1)}, u32[]{:S(2)}, u32[]{:S(2)}) async-start(f32[4,1,11540]{2,1,0:T(1,128)} %broadcast_in_dim.82), calls=%async_computation | async-start | bytes 372736 | tf_op jit(solution)/shard_map/all_to_all | solution.py:11
  32.5 90.0 %all-gather.3.cloned.1.call-start = ((), (), s32[]{:S(2)}) async-start(), calls=%async_computation.4 | async-start | bytes 1996800 | tf_op jit(solution)/shard_map/all_gather | solution.py:148
  42.7 10.4 %all-to-all-start.1 = ((f32[4,2,128,128]{3,1,2,0:T(2,128)}), f32[4,2,128,128]{3,1,2,0:T(2,128)S(1)}, u32[]{:S(2)}, u32[]{:S(2)}) async-start(f32[4,2,128,128]{3,1,2,0:T(2,128)} %fusion.26), calls=%async_computation.1 | async-start | bytes 1048576 | tf_op jit(solution)/shard_map/all_to_all | solution.py:135
  87.5 25.9 %all-to-all-start.3 = ((f32[64,16,128]{2,1,0:T(8,128)}), f32[64,16,128]{2,1,0:T(8,128)S(1)}, u32[]{:S(2)}, u32[]{:S(2)}) async-start(f32[64,16,128]{2,1,0:T(8,128)} %broadcast_in_dim.84), calls=%async_computation.3 | async-start | bytes 1048576 | tf_op jit(solution)/shard_map/all_to_all | solution.py:11
Sparse Core Ops, SparseCore 0:
  40.9 81.6 all-gather.2
where the time goes:
time: 137 us
  waiting for transfers between devices  38.5 us (28%)
  blocking collectives  32.6 us (24%)
  local copies, waits for them, and re-layouts  23.2 us (17%)
  starting transfers between devices  14.6 us (11%)
  between operations  14.3 us (10%)
  matrix products  10.7 us (8%)
  other arithmetic  2.98 us (2%)
    all_to_all x1, blocking collectives, sent_and_summed(): pieces = lax.all_to_all(split_up(x, dim, count), axis, 0, 0, tiled=True)  32.6 us
    all_to_all x2, waiting for transfers between devices, sent_to_all(): lax.all_to_all(jnp.broadcast_to(x[None], (count, *x.shape)), axis, 0, 0,...  23.6 us
    all_to_all x2, starting transfers between devices, sent_to_all(): lax.all_to_all(jnp.broadcast_to(x[None], (count, *x.shape)), axis, 0, 0,...  11.1 us
    all_gather x1, waiting for transfers between devices, shards(): portion = lax.all_gather(fitted, 'aux', axis=0, tiled=True)  9.23 us
    unnamed x10, local copies, waits for them, and re-layouts  7.98 us
    all_to_all x1, waiting for transfers between devices, shards(): lax.all_to_all(outbound, 'pair', split_axis=0, concat_axis=0, tiled=True)  5.68 us
    all_to_all x1, starting transfers between devices, shards(): lax.all_to_all(outbound, 'pair', split_axis=0, concat_axis=0, tiled=True)  3.47 us
    dot_general x1, matrix products, fitted_terms(): jnp.einsum('rpab,rab->p', blocks, density, preferred_element_type=jnp.flo...  2.98 us
  transfers between devices with their start and end apart: 4, of which 4 were waited for; matrix products, arithmetic and copies ran while one was open for 4% of the time, Pallas kernels for 0%

commit v1 on v0

v1 whole, which is shorter than its diff:
```python
import math

import jax
import jax.numpy as jnp
from jax import lax
from jax.experimental import pallas as pl
from jax.experimental.pallas import tpu as pltpu
from jax.sharding import Mesh, PartitionSpec as P

SLOTS = 4
ROWS = 20
BW = 128
ACT = 24
PAIRS = 576
GROUPS = 4
PER = 5
USED = PER * ACT
CHIPS = 32
CORES = 2
OWNERS = 4
AUX = 1280
MSG = 24
F32 = jnp.float32
BF16 = jnp.bfloat16

ANY = pl.BlockSpec(memory_space=pl.ANY)
VMEM = pl.BlockSpec(memory_space=pltpu.VMEM)
SMEM = pl.BlockSpec(memory_space=pltpu.SMEM)


def nt(a, b):
    return lax.dot_general(a, b, (((1,), (1,)), ((), ())), preferred_element_type=F32)


def lanes(shape):
    return lax.broadcasted_iota(jnp.int32, shape, len(shape) - 1)


def sublanes(shape):
    return lax.broadcasted_iota(jnp.int32, shape, len(shape) - 2)


def contract_kernel(
    mask_ref, index_ref, blocks_hbm, active_hbm, inactive_hbm, out_ref,
    blocks, act_row, act_col, ina_row, ina_col, wide, halves, sums,
    block_sem, ar_sem, ac_sem, ir_sem, ic_sem,
):
    here = lax.axis_index("pair")
    copies = []
    for g in range(SLOTS):
        slot = here * SLOTS + g
        row = pl.multiple_of(index_ref[0, slot] * BW, BW)
        col = pl.multiple_of(index_ref[1, slot] * BW, BW)
        group = [
            pltpu.make_async_copy(inactive_hbm.at[:, pl.ds(row, BW)], ina_row.at[g], ir_sem.at[g]),
            pltpu.make_async_copy(inactive_hbm.at[:, pl.ds(col, BW)], ina_col.at[g], ic_sem.at[g]),
            pltpu.make_async_copy(active_hbm.at[:, pl.ds(row, BW)], act_row.at[g], ar_sem.at[g]),
            pltpu.make_async_copy(active_hbm.at[:, pl.ds(col, BW)], act_col.at[g], ac_sem.at[g]),
            pltpu.make_async_copy(blocks_hbm.at[g], blocks.at[g], block_sem.at[g]),
        ]
        for c in group:
            c.start()
        copies.append(group)
    wide[...] = jnp.zeros_like(wide)
    for g in range(SLOTS):
        live = mask_ref[here * SLOTS + g].astype(F32)
        for c in copies[g]:
            c.wait()
        density = lax.dot_general(
            ina_row[g], ina_col[g], (((0,), (0,)), ((), ())), preferred_element_type=F32
        )
        density = density.astype(BF16).astype(F32) * live
        for p in range(ROWS):
            product = blocks[g, p].astype(F32) * density
            part = jnp.sum(product.reshape(BW // 8, 8, BW), axis=0)
            if g == 0:
                sums[p] = part
            else:
                sums[p] = sums[p] + part
        column = act_col[g].astype(F32)
        for p in range(PER):
            wide[pl.ds(ACT * p, ACT), pl.ds(BW * p, BW)] = column
        weights = wide[...].astype(BF16)
        for k in range(GROUPS):
            joined = jnp.concatenate([blocks[g, k * PER + p] for p in range(PER)], axis=1)
            half = nt(joined, weights)
            halves[pl.ds(g * BW, BW), pl.ds(k * BW, BW)] = half.astype(BF16)
    rows = jnp.concatenate(
        [
            act_row[g].astype(F32) * mask_ref[here * SLOTS + g].astype(F32)
            for g in range(SLOTS)
        ],
        axis=1,
    ).astype(BF16)
    fitted = jnp.dot(rows, halves[...], preferred_element_type=F32)
    coupling = jnp.sum(jnp.sum(sums[...], axis=1), axis=1, keepdims=True) * (1.0 / BW)
    coupling = jnp.concatenate([coupling, jnp.zeros((ACT - ROWS, 1), F32)], axis=0)
    high = coupling.astype(BF16).astype(F32)
    low = coupling - high
    spare = lanes((ACT, BW)) >= USED
    for k in range(GROUPS):
        tail = high if k == 0 else low if k == 1 else jnp.zeros_like(high)
        tile = jnp.where(spare, jnp.broadcast_to(tail, (ACT, BW)), fitted[:, k * BW : (k + 1) * BW])
        out_ref[:, pl.ds(k * BW, BW)] = tile.astype(BF16)


def expand_kernel(
    own_ref, one_ref, two_ref, three_ref, blocks_hbm, keep_ref, send_ref,
    blocks, coupling_ref, spread, left, coulomb, main, rest, block_sem,
):
    here = lax.axis_index("pair")
    core = lax.axis_index("core")
    copies = [
        pltpu.make_async_copy(blocks_hbm.at[g], blocks.at[g], block_sem.at[g]) for g in range(SLOTS)
    ]
    for c in copies:
        c.start()
    total = (own_ref[...].astype(F32) + two_ref[...].astype(F32)) + (
        one_ref[...].astype(F32) + three_ref[...].astype(F32)
    )
    both = total[:, :BW] + total[:, BW : 2 * BW]
    coupling = jnp.sum(jnp.where(lanes((ACT, BW)) == USED, both, 0.0), axis=1, keepdims=True)
    coupling_ref[...] = jnp.broadcast_to(coupling.astype(BF16).astype(F32), (ACT, BW))
    fitted = total.astype(BF16).astype(F32)
    offset = lanes((ACT, BW)) - sublanes((ACT, BW))
    keep = offset == 0
    for p in range(1, PER):
        keep = keep | (offset == ACT * p)
    keep = jnp.concatenate([keep.astype(F32)] * GROUPS, axis=1)
    for t in range(0, ACT, 2):
        pair = jnp.concatenate(
            [jnp.broadcast_to(fitted[t + d : t + d + 1, :], keep.shape) * keep for d in range(2)],
            axis=0,
        )
        spread[pl.ds(t * ACT, 2 * ACT), :] = pair.astype(BF16)
    shape = (GROUPS * BW, BW)
    lane = lanes(shape)
    group = (
        (lane >= PER).astype(jnp.int32)
        + (lane >= 2 * PER).astype(jnp.int32)
        + (lane >= 3 * PER).astype(jnp.int32)
    )
    start = group * BW + (lane - group * PER) * ACT
    position = sublanes(shape) - start
    pick = (position >= 0) & (position < ACT) & (lane < ROWS)
    folded = jnp.dot(
        spread[...], pick.astype(F32).astype(BF16), preferred_element_type=F32
    ).astype(BF16)
    left[...] = folded
    columns = left[pl.ds(pl.multiple_of(here * BW, BW), BW), :]
    tail = left[pl.ds(4 * BW, PAIRS - 4 * BW), :]
    main[...] = nt(folded, columns)
    rest[...] = nt(folded, jnp.concatenate([tail, tail], axis=0))
    for g in range(SLOTS):
        copies[g].wait()
        total_g = jnp.zeros((BW, BW), F32)
        for p in range(ROWS):
            factor = jnp.broadcast_to(coupling_ref[pl.ds(p, 1), :], (BW, BW))
            total_g = total_g + blocks[g, p].astype(F32) * factor
        coulomb[pl.ds(g * BW, BW), :] = total_g
    low_lane = lanes((CHIPS, BW)) < BW // 2
    for ref, which in ((keep_ref, core), (send_ref, 1 - core)):
        for g in range(SLOTS):
            for s in range(2):
                value = coulomb[pl.ds(g * BW + s * (BW // 2) + which, CHIPS, stride=2), :]
                ref[pl.ds(2 * g + s, CHIPS, stride=MSG), :] = value
        for s in range(9):
            ref[pl.ds(8 + s, CHIPS, stride=MSG), :] = main[pl.ds(9 * which + s, CHIPS, stride=18), :]
        for s in range(7):
            value = rest[pl.ds(9 * which + s, CHIPS, stride=18), :]
            if s < 2:
                other = rest[pl.ds(9 * which + 7 + s, CHIPS, stride=18), :]
                value = jnp.where(low_lane, value, other)
            ref[pl.ds(17 + s, CHIPS, stride=MSG), :] = value


def route_kernel(mask_ref, owner_ref, parts_ref, out_ref, gram_ref, tile):
    here = lax.axis_index("pair")
    total = jnp.sum(parts_ref[...].astype(F32), axis=0)
    gram_ref[...] = total[8:MSG] * (1.0 / AUX)
    scaled = total[0:8] * (1.0 / math.sqrt(AUX))
    tile[...] = jnp.zeros_like(tile)
    for o in range(OWNERS):
        place = jnp.int32(0)
        for g in range(SLOTS):
            slot = here * SLOTS + g
            chosen = (mask_ref[slot] == 1) & (owner_ref[slot] == o)

            @pl.when(chosen & (place < 2))
            def _(o=o, g=g, place=place):
                tile[o, pl.ds(2 * place, 2), :] = scaled[2 * g : 2 * g + 2]

            place = place + chosen.astype(jnp.int32)
    for o in range(OWNERS):
        piece = tile[o, 0:4, :]
        many = jnp.broadcast_to(piece[None], (CHIPS, 4, BW)).reshape(CHIPS * 4, BW)
        out_ref[pl.ds(o * CHIPS * 4, CHIPS * 4), :] = many.astype(BF16)


def place_kernel(
    mask_ref, owner_ref, own_ref, other_ref, g0_ref, g1_ref, g2_ref, g3_ref,
    fock_ref, gram_ref, wide,
):
    here = lax.axis_index("pair")
    core = lax.axis_index("core")
    fock_ref[...] = jnp.zeros_like(fock_ref)
    wide[0] = own_ref[...].astype(F32)
    wide[1] = other_ref[...].astype(F32)
    rank = jnp.int32(0)
    for q in range(OWNERS):
        place = jnp.int32(0)
        for g in range(SLOTS):
            slot = q * SLOTS + g
            chosen = (mask_ref[slot] == 1) & (owner_ref[slot] == here)

            @pl.when(chosen & (place < 2))
            def _(q=q, rank=rank, place=place):
                for n in range(2):
                    which = core if n == 0 else 1 - core
                    for s in range(2):
                        value = wide[n, pl.ds(q * CHIPS * 4 + 2 * place + s, CHIPS, stride=4), :]
                        fock_ref[pl.ds(rank * BW + s * (BW // 2) + which, CHIPS, stride=2), :] = value

            place = place + chosen.astype(jnp.int32)
            rank = rank + chosen.astype(jnp.int32)
    for n, ref in enumerate((g0_ref, g1_ref, g2_ref, g3_ref)):
        source = lax.rem(here + OWNERS - n, OWNERS)
        gram_ref[:, pl.ds(pl.multiple_of(source * BW, BW), BW)] = ref[0:9, :]
    gram_ref[0:7, pl.ds(4 * BW, BW // 2)] = g0_ref[9:16, 0 : BW // 2]
    gram_ref[7:9, pl.ds(4 * BW, BW // 2)] = g0_ref[9:11, BW // 2 : BW]


def from_others(x):
    return [
        lax.ppermute(x, "pair", [(i, (i + s) % OWNERS) for i in range(OWNERS)])
        for s in range(1, OWNERS)
    ]


def shards(three_centre, block_mask, block_owner, block_index, active_orbitals, inactive_orbitals):
    dma = pltpu.SemaphoreType.DMA
    message = pl.pallas_call(
        contract_kernel,
        out_shape=jax.ShapeDtypeStruct((ACT, GROUPS * BW), BF16),
        in_specs=[SMEM, SMEM, ANY, ANY, ANY],
        out_specs=VMEM,
        scratch_shapes=[
            pltpu.VMEM((SLOTS, ROWS, BW, BW), BF16),
            pltpu.VMEM((SLOTS, ACT, BW), BF16),
            pltpu.VMEM((SLOTS, ACT, BW), BF16),
            pltpu.VMEM((SLOTS, 256, BW), BF16),
            pltpu.VMEM((SLOTS, 256, BW), BF16),
            pltpu.VMEM((BW, PER * BW), F32),
            pltpu.VMEM((SLOTS * BW, GROUPS * BW), BF16),
            pltpu.VMEM((ROWS, 8, BW), F32),
            dma((SLOTS,)), dma((SLOTS,)), dma((SLOTS,)), dma((SLOTS,)), dma((SLOTS,)),
        ],
        name="contract",
    )(block_mask, block_index, three_centre, active_orbitals, inactive_orbitals)
    one, two, three = from_others(message)
    rows = CHIPS * MSG
    keep, send = pl.pallas_call(
        expand_kernel,
        out_shape=[jax.ShapeDtypeStruct((rows, BW), F32)] * 2,
        in_specs=[VMEM, VMEM, VMEM, VMEM, ANY],
        out_specs=[VMEM, VMEM],
        scratch_shapes=[
            pltpu.VMEM((SLOTS, ROWS, BW, BW), BF16),
            pltpu.VMEM((ACT, BW), F32),
            pltpu.VMEM((PAIRS, GROUPS * BW), BF16),
            pltpu.VMEM((PAIRS, BW), BF16),
            pltpu.VMEM((SLOTS * BW, BW), F32),
            pltpu.VMEM((PAIRS, BW), F32),
            pltpu.VMEM((PAIRS, BW), F32),
            dma((SLOTS,)),
        ],
        name="expand",
    )(message, one, two, three, three_centre)
    swap = [(0, 1), (1, 0)]
    chip_sum = (keep + lax.ppermute(send, "core", swap)).astype(BF16)
    parts = lax.all_to_all(chip_sum.reshape(CHIPS, MSG, BW), "chip", 0, 0, tiled=True)
    pieces, gram = pl.pallas_call(
        route_kernel,
        out_shape=[
            jax.ShapeDtypeStruct((OWNERS * CHIPS * 4, BW), BF16),
            jax.ShapeDtypeStruct((16, BW), F32),
        ],
        in_specs=[SMEM, SMEM, VMEM],
        out_specs=[VMEM, VMEM],
        scratch_shapes=[pltpu.VMEM((OWNERS, 8, BW), F32)],
        name="route",
    )(block_mask, block_owner, parts)
    g1, g2, g3 = from_others(gram)
    received = lax.all_to_all(
        pieces.reshape(OWNERS * CHIPS, 4, BW), ("pair", "chip"), 0, 0, tiled=True
    ).reshape(OWNERS * CHIPS * 4, BW)
    partner = lax.ppermute(received, "core", swap)
    fock, integrals = pl.pallas_call(
        place_kernel,
        out_shape=[
            jax.ShapeDtypeStruct((8 * BW, BW), F32),
            jax.ShapeDtypeStruct((9, PAIRS), F32),
        ],
        in_specs=[SMEM, SMEM] + [VMEM] * 6,
        out_specs=[VMEM, VMEM],
        scratch_shapes=[pltpu.VMEM((2, OWNERS * CHIPS * 4, BW), F32)],
        name="place",
    )(block_mask, block_owner, received, partner, gram, g1, g2, g3)
    return (fock.reshape(8, BW, BW), integrals)


def solution(mesh):
    split = Mesh(mesh.devices.reshape(CHIPS, CORES, OWNERS), ("chip", "core", "pair"))
    return jax.shard_map(
        shards,
        mesh=split,
        in_specs=(P("pair", ("chip", "core"), None, None), P(), P(), P(), P(), P()),
        out_specs=(P("pair", None, None), P(("chip", "core"), None)),
        check_vma=False,
    )
```

time: 137 us -> 76.2 us (0.56)
  waiting for transfers between devices: 38.5 us -> 8.99 us
  local copies, waits for them, and re-layouts: 23.2 us -> 2.19 us
  between operations: 14.3 us -> 0.68 us
  Pallas kernels: 0 us -> 12 us
  matrix products: 10.7 us -> 0 us
  blocking collectives: 32.6 us -> 39.9 us
  starting transfers between devices: 14.6 us -> 11 us
  other arithmetic: 2.98 us -> 1.07 us
    all_to_all x3 -> x0, waiting for transfers between devices: 29.2 us -> none  [the longest x2 23.6 us: sent_to_all(): lax.all_to_all(jnp.broadcast_to(x[None], (count, *x.shape)), axis, 0, 0,...]
    all_to_all x3 -> x0, starting transfers between devices: 14.6 us -> none  [the longest x2 11.1 us: sent_to_all(): lax.all_to_all(jnp.broadcast_to(x[None], (count, *x.shape)), axis, 0, 0,...]
    pallas_call x0 -> x4, Pallas kernels: none -> 12 us  [the longest x1 4.51 us: shards(): pl.pallas_call(contract_kernel, out_shape=jax.ShapeDtypeStruct((ACT, GROU...]
    ppermute x0 -> x8, starting transfers between devices: none -> 11 us  [the longest x6 6.46 us: from_others(): lax.ppermute(x, 'pair', [(i, (i + s) % OWNERS) for i in range(OWNERS)])]
    dot_general x6 -> x0, matrix products: 10.7 us -> none  [the longest x1 2.98 us: fitted_terms(): jnp.einsum('rpab,rab->p', blocks, density, preferred_element_type=jnp.flo...]
    all_gather x1 -> x0, waiting for transfers between devices: 9.23 us -> none  [shards(): portion = lax.all_gather(fitted, 'aux', axis=0, tiled=True)]
    ppermute x0 -> x8, waiting for transfers between devices: none -> 8.99 us  [the longest x6 7.43 us: from_others(): lax.ppermute(x, 'pair', [(i, (i + s) % OWNERS) for i in range(OWNERS)])]
    gather x9 -> x0, local copies, waits for them, and re-layouts: 8.28 us -> none  [the longest x1 2 us: fitted_terms(): inactive_rows = jnp.take(inactive_split, row_blocks, axis=1)]
  transfers between devices with their start and end apart: 4 -> 8, of which waited for: 4 -> 7; matrix products, arithmetic and copies ran while one was open for 4% -> 0% of each run, Pallas kernels for 0% -> 0%
where the time goes in v1:
time: 76.2 us; the launch traced here: 75.8 us
  blocking collectives  39.9 us (52%)
  Pallas kernels  12 us (16%)
  starting transfers between devices  11 us (14%)
  waiting for transfers between devices  8.99 us (12%)
  local copies, waits for them, and re-layouts  2.19 us (3%)
  other arithmetic  1.07 us (1%)
    all_to_all x1, blocking collectives, shards(): lax.all_to_all(chip_sum.reshape(CHIPS, MSG, BW), 'chip', 0, 0, tiled=True)  20.3 us
    all_to_all x1, blocking collectives, shards(): lax.all_to_all(pieces.reshape(OWNERS * CHIPS, 4, BW), ('pair', 'chip'), 0...  19.6 us
    ppermute x6, waiting for transfers between devices, from_others(): lax.ppermute(x, 'pair', [(i, (i + s) % OWNERS) for i in range(OWNERS)])  7.43 us
    ppermute x6, starting transfers between devices, from_others(): lax.ppermute(x, 'pair', [(i, (i + s) % OWNERS) for i in range(OWNERS)])  6.46 us
    pallas_call x1, Pallas kernels, shards(): pl.pallas_call(contract_kernel, out_shape=jax.ShapeDtypeStruct((ACT, GROU...  4.51 us
    pallas_call x1, Pallas kernels, shards(): pl.pallas_call(expand_kernel, out_shape=[jax.ShapeDtypeStruct((rows, BW),...  3.63 us
    ppermute x1, starting transfers between devices, shards(): partner = lax.ppermute(received, 'core', swap)  2.41 us
    unnamed x16, local copies, waits for them, and re-layouts  2.19 us
  transfers between devices with their start and end apart: 8, of which 7 were waited for; matrix products, arithmetic and copies ran while one was open for 0% of the time, Pallas kernels for 0%

profile of v1, /device:TPU:1, one launch (start us, length us, event | category | flops | bytes accessed | tf_op | source)
XLA Modules:
  0.0 75.8 jit_solution(11582119156920726447)
XLA Ops:
  0.6 4.5 %contract.1.own_ref = bf16[24,512]{1,0:T(8,128)(2,1)} custom-call(s32[16]{0:T(128)} %mask_ref.5, s32[2,16]{1,0:T(2,128)} %index_ref.1, bf16[4,20,128,128]{3,2,1,0:T(8,128)(2,1)} %blocks_hbm.3, bf16[24,3072]{1,0:T(8,128)(2,1)} %active_hbm.1, bf16[256,3072]{1,0:T(8,128)(2,1)} %inactive_hbm.1), custom_call_target="tpu_custom_call" | custom-call | tf_op jit(solution)/shard_map/contract/pallas_call | solution.py:242
  5.1 3.6 %collective-permute-start.2 = (bf16[24,512]{1,0:T(8,128)(2,1)}, bf16[24,512]{1,0:T(8,128)(2,1)S(1)}, u32[]{:S(2)}, u32[]{:S(2)}) collective-permute-start(bf16[24,512]{1,0:T(8,128)(2,1)} %contract.1.own_ref), channel_id=1, source_target_pairs={{0,3},{1,0},{2,1},{3,2},{4,7},{5,4},{6,5},{7,6},{8,11},{9,8},{10,9... | collective-permute-start | bytes 73736 | tf_op jit(solution)/shard_map/ppermute | solution.py:235
  8.8 0.3 collective-permute-start.1
  9.1 0.7 collective-permute-start
  9.8 0.1 collective-permute-done.2.three_ref
  9.9 0.0 copy-start.2
  9.9 3.2 %collective-permute-done.1.two_ref = bf16[24,512]{1,0:T(8,128)(2,1)S(1)} collective-permute-done((bf16[24,512]{1,0:T(8,128)(2,1)}, bf16[24,512]{1,0:T(8,128)(2,1)S(1)}, u32[]{:S(2)}, u32[]{:S(2)}) %collective-permute-start.1) | collective-permute-done | bytes 24608 | tf_op jit(solution)/shard_map/ppermute | solution.py:235
  13.2 0.0 copy-start.3
  13.2 0.2 collective-permute-done.one_ref
  13.4 0.0 copy-done.2
  13.4 0.3 copy-done.3
  13.8 0.0 copy-start.4
  13.8 0.6 copy-done.4
  14.4 3.6 %expand.1 = (f32[768,128]{1,0:T(8,128)}, f32[768,128]{1,0:T(8,128)}) custom-call(bf16[24,512]{1,0:T(8,128)(2,1)} %contract.1.own_ref, bf16[24,512]{1,0:T(8,128)(2,1)} %copy-done.4, bf16[24,512]{1,0:T(8,128)(2,1)} %copy-done.3, bf16[24,512]{1,0:T(8,128)(2,1)} %copy-done.2, bf16[4,20,128,128]{3,2,1,0:T(8,128)(2,1)} %blocks_hbm.3), custom_call_target="tpu_custom_call" | custom-call | tf_op jit(solution)/shard_map/expand/pallas_call | solution.py:262
  18.0 2.2 %collective-permute-start.3 = (f32[768,128]{1,0:T(8,128)}, f32[768,128]{1,0:T(8,128)S(1)}, u32[]{:S(2)}, u32[]{:S(2)}) collective-permute-start(f32[768,128]{1,0:T(8,128)} %get-tuple-element.9), channel_id=1, source_target_pairs={{0,4},{4,0},{1,5},{5,1},{2,6},{6,2},{3,7},{7,3},{8,12},{12,8},{9,1... | collective-permute-start | bytes 1179656 | tf_op jit(solution)/shard_map/ppermute | solution.py:280
  20.2 1.6 %collective-permute-done.3 = f32[768,128]{1,0:T(8,128)S(1)} collective-permute-done((f32[768,128]{1,0:T(8,128)}, f32[768,128]{1,0:T(8,128)S(1)}, u32[]{:S(2)}, u32[]{:S(2)}) %collective-permute-start.3) | collective-permute-done | bytes 393248 | tf_op jit(solution)/shard_map/ppermute | solution.py:280
  21.8 1.1 %add_convert_fusion = bf16[768,128]{1,0:T(8,128)(2,1)S(1)} fusion(f32[768,128]{1,0:T(8,128)} %get-tuple-element.8, f32[768,128]{1,0:T(8,128)S(1)} %collective-permute-done.3), kind=kLoop, calls=%fused_computation | loop fusion | flops 196608 | bytes 983040 | tf_op jit(solution)/shard_map/convert_element_type | solution.py:280
  22.8 20.3 %all_to_all.10.parts_ref = bf16[32,24,128]{2,1,0:T(8,128)(2,1)} all-to-all(bf16[32,24,128]{2,1,0:T(8,128)(2,1)S(1)} %bitcast.4), channel_id=1, replica_groups=mesh['chip'=32,'core'=2,'pair'=4] {'chip'}, dimensions={0} | all-to-all | bytes 393216 | tf_op jit(solution)/shard_map/all_to_all | solution.py:281
  43.2 1.8 %route.1 = (bf16[512,128]{1,0:T(8,128)(2,1)}, f32[16,128]{1,0:T(8,128)}) custom-call(s32[16]{0:T(128)} %mask_ref.5, s32[16]{0:T(128)} %owner_ref.3, bf16[32,24,128]{2,1,0:T(8,128)(2,1)} %all_to_all.10.parts_ref), custom_call_target="tpu_custom_call" | custom-call | tf_op jit(solution)/shard_map/route/pallas_call | solution.py:282
  45.0 19.6 %all_to_all.11 = bf16[128,4,128]{2,1,0:T(4,128)(2,1)S(1)} all-to-all(bf16[128,4,128]{2,1,0:T(4,128)(2,1)} %bitcast.7), channel_id=1, replica_groups=mesh['chip'=32,'core'=2,'pair'=4] {'pair','chip'}, dimensions={0} | all-to-all | bytes 262144 | tf_op jit(solution)/shard_map/all_to_all | solution.py:294
  64.5 0.0 copy-start
  64.5 2.4 %collective-permute-start.4 = (bf16[512,128]{1,0:T(8,128)(2,1)S(1)}, bf16[512,128]{1,0:T(8,128)(2,1)S(1)}, u32[]{:S(2)}, u32[]{:S(2)}) collective-permute-start(bf16[512,128]{1,0:T(8,128)(2,1)S(1)} %bitcast.5), channel_id=1, source_target_pairs={{0,4},{4,0},{1,5},{5,1},{2,6},{6,2},{3,7},{7,3},{8,12},{12,8},{9,1... | collective-permute-start | bytes 393224 | tf_op jit(solution)/shard_map/ppermute | solution.py:297
  67.0 0.4 collective-permute-start.7
  67.3 1.3 %collective-permute-start.6 = (f32[16,128]{1,0:T(8,128)}, f32[16,128]{1,0:T(8,128)S(1)}, u32[]{:S(2)}, u32[]{:S(2)}) collective-permute-start(f32[16,128]{1,0:T(8,128)} %get-tuple-element.11.g0_ref), channel_id=1, source_target_pairs={{0,2},{1,3},{2,0},{3,1},{4,6},{5,7},{6,4},{7,5},{8,10},{9,11},{10,... | collective-permute-start | bytes 24584 | tf_op jit(solution)/shard_map/ppermute | solution.py:235
  68.6 0.1 collective-permute-start.5
  68.7 0.9 %collective-permute-done.7.g3_ref = f32[16,128]{1,0:T(8,128)S(1)} collective-permute-done((f32[16,128]{1,0:T(8,128)}, f32[16,128]{1,0:T(8,128)S(1)}, u32[]{:S(2)}, u32[]{:S(2)}) %collective-permute-start.7) | collective-permute-done | bytes 8224 | tf_op jit(solution)/shard_map/ppermute | solution.py:235
  69.7 0.0 copy-start.5
  69.7 1.9 %collective-permute-done.6.g2_ref = f32[16,128]{1,0:T(8,128)S(1)} collective-permute-done((f32[16,128]{1,0:T(8,128)}, f32[16,128]{1,0:T(8,128)S(1)}, u32[]{:S(2)}, u32[]{:S(2)}) %collective-permute-start.6) | collective-permute-done | bytes 8224 | tf_op jit(solution)/shard_map/ppermute | solution.py:235
  71.5 0.0 copy-start.6
  71.5 1.0 %collective-permute-done.5.g1_ref = f32[16,128]{1,0:T(8,128)S(1)} collective-permute-done((f32[16,128]{1,0:T(8,128)}, f32[16,128]{1,0:T(8,128)S(1)}, u32[]{:S(2)}, u32[]{:S(2)}) %collective-permute-start.5) | collective-permute-done | bytes 8224 | tf_op jit(solution)/shard_map/ppermute | solution.py:235
  72.6 0.0 copy-start.7
  72.6 0.0 collective-permute-done.4.other_ref
  72.6 0.0 copy-done
  72.6 0.0 copy-done.5
  72.6 0.0 copy-done.6
  72.6 0.6 copy-done.7
  73.2 0.0 copy-start.1
  73.2 0.7 copy-done.1
  73.8 2.0 %place.1 = (f32[1024,128]{1,0:T(8,128)}, f32[9,576]{1,0:T(8,128)}) custom-call(s32[16]{0:T(128)} %mask_ref.5, s32[16]{0:T(128)} %owner_ref.3, bf16[512,128]{1,0:T(8,128)(2,1)} %bitcast.6, bf16[512,128]{1,0:T(8,128)(2,1)} %copy-done.1, f32[16,128]{1,0:T(8,128)} %get-tuple-element.11.g0_ref, f32[16,128]{1,0:T(8,128)} %copy-done.7, f32[16,128]{1,0:T(8,128)} %copy-done.6, ...), custom_call_target="tpu_custom_call" | custom-call | tf_op jit(solution)/shard_map/place/pallas_call | solution.py:298
Async XLA Ops:
  5.1 4.8 %collective-permute-start.2 = (bf16[24,512]{1,0:T(8,128)(2,1)}, bf16[24,512]{1,0:T(8,128)(2,1)S(1)}, u32[]{:S(2)}, u32[]{:S(2)}) collective-permute-start(bf16[24,512]{1,0:T(8,128)(2,1)} %contract.1.own_ref), channel_id=1, source_target_pairs={{0,3},{1,0},{2,1},{3,2},{4,7},{5,4},{6,5},{7,6},{8,11},{9,8},{10,9... | collective-permute-start | bytes 73736 | tf_op jit(solution)/shard_map/ppermute | solution.py:235
  8.8 4.4 %collective-permute-start.1 = (bf16[24,512]{1,0:T(8,128)(2,1)}, bf16[24,512]{1,0:T(8,128)(2,1)S(1)}, u32[]{:S(2)}, u32[]{:S(2)}) collective-permute-start(bf16[24,512]{1,0:T(8,128)(2,1)} %contract.1.own_ref), channel_id=1, source_target_pairs={{0,2},{1,3},{2,0},{3,1},{4,6},{5,7},{6,4},{7,5},{8,10},{9,11},{10,... | collective-permute-start | bytes 73736 | tf_op jit(solution)/shard_map/ppermute | solution.py:235
  9.1 4.3 %collective-permute-start = (bf16[24,512]{1,0:T(8,128)(2,1)}, bf16[24,512]{1,0:T(8,128)(2,1)S(1)}, u32[]{:S(2)}, u32[]{:S(2)}) collective-permute-start(bf16[24,512]{1,0:T(8,128)(2,1)} %contract.1.own_ref), channel_id=1, source_target_pairs={{0,1},{1,2},{2,3},{3,0},{4,5},{5,6},{6,7},{7,4},{8,9},{9,10},{10,1... | collective-permute-start | bytes 73736 | tf_op jit(solution)/shard_map/ppermute | solution.py:235
  9.9 3.5 %copy-start.2 = (bf16[24,512]{1,0:T(8,128)(2,1)}, bf16[24,512]{1,0:T(8,128)(2,1)S(1)}, u32[]{:S(2)}) copy-start(bf16[24,512]{1,0:T(8,128)(2,1)S(1)} %collective-permute-done.2.three_ref) | copy-start | bytes 73732
  13.2 0.6 copy-start.3
  13.8 0.6 copy-start.4
  18.0 3.7 %collective-permute-start.3 = (f32[768,128]{1,0:T(8,128)}, f32[768,128]{1,0:T(8,128)S(1)}, u32[]{:S(2)}, u32[]{:S(2)}) collective-permute-start(f32[768,128]{1,0:T(8,128)} %get-tuple-element.9), channel_id=1, source_target_pairs={{0,4},{4,0},{1,5},{5,1},{2,6},{6,2},{3,7},{7,3},{8,12},{12,8},{9,1... | collective-permute-start | bytes 1179656 | tf_op jit(solution)/shard_map/ppermute | solution.py:280
  64.5 8.0 %copy-start = (bf16[128,4,128]{2,1,0:T(4,128)(2,1)}, bf16[128,4,128]{2,1,0:T(4,128)(2,1)S(1)}, u32[]{:S(2)}) copy-start(bf16[128,4,128]{2,1,0:T(4,128)(2,1)S(1)} %all_to_all.11) | copy-start | bytes 393220
  64.5 8.0 %collective-permute-start.4 = (bf16[512,128]{1,0:T(8,128)(2,1)S(1)}, bf16[512,128]{1,0:T(8,128)(2,1)S(1)}, u32[]{:S(2)}, u32[]{:S(2)}) collective-permute-start(bf16[512,128]{1,0:T(8,128)(2,1)S(1)} %bitcast.5), channel_id=1, source_target_pairs={{0,4},{4,0},{1,5},{5,1},{2,6},{6,2},{3,7},{7,3},{8,12},{12,8},{9,1... | collective-permute-start | bytes 393224 | tf_op jit(solution)/shard_map/ppermute | solution.py:297
  67.0 2.7 %collective-permute-start.7 = (f32[16,128]{1,0:T(8,128)}, f32[16,128]{1,0:T(8,128)S(1)}, u32[]{:S(2)}, u32[]{:S(2)}) collective-permute-start(f32[16,128]{1,0:T(8,128)} %get-tuple-element.11.g0_ref), channel_id=1, source_target_pairs={{0,3},{1,0},{2,1},{3,2},{4,7},{5,4},{6,5},{7,6},{8,11},{9,8},{10,9... | collective-permute-start | bytes 24584 | tf_op jit(solution)/shard_map/ppermute | solution.py:235
  67.3 4.2 %collective-permute-start.6 = (f32[16,128]{1,0:T(8,128)}, f32[16,128]{1,0:T(8,128)S(1)}, u32[]{:S(2)}, u32[]{:S(2)}) collective-permute-start(f32[16,128]{1,0:T(8,128)} %get-tuple-element.11.g0_ref), channel_id=1, source_target_pairs={{0,2},{1,3},{2,0},{3,1},{4,6},{5,7},{6,4},{7,5},{8,10},{9,11},{10,... | collective-permute-start | bytes 24584 | tf_op jit(solution)/shard_map/ppermute | solution.py:235
  68.6 3.9 %collective-permute-start.5 = (f32[16,128]{1,0:T(8,128)}, f32[16,128]{1,0:T(8,128)S(1)}, u32[]{:S(2)}, u32[]{:S(2)}) collective-permute-start(f32[16,128]{1,0:T(8,128)} %get-tuple-element.11.g0_ref), channel_id=1, source_target_pairs={{0,1},{1,2},{2,3},{3,0},{4,5},{5,6},{6,7},{7,4},{8,9},{9,10},{10,1... | collective-permute-start | bytes 24584 | tf_op jit(solution)/shard_map/ppermute | solution.py:235
  69.7 2.9 %copy-start.5 = (f32[16,128]{1,0:T(8,128)}, f32[16,128]{1,0:T(8,128)S(1)}, u32[]{:S(2)}) copy-start(f32[16,128]{1,0:T(8,128)S(1)} %collective-permute-done.7.g3_ref) | copy-start | bytes 24580
  71.5 1.1 %copy-start.6 = (f32[16,128]{1,0:T(8,128)}, f32[16,128]{1,0:T(8,128)S(1)}, u32[]{:S(2)}) copy-start(f32[16,128]{1,0:T(8,128)S(1)} %collective-permute-done.6.g2_ref) | copy-start | bytes 24580
  72.6 0.6 copy-start.7
  73.2 0.7 copy-start.1
